TPU v7x, 512 devices: a whole 4x8x8 slice. The times are simulated.
512 devices in a mesh: fsdp: 64 (over x, y, core), dp: 8 (over z).
Axes of the slice: x: 4, y: 8, z: 8, core: 2. Of those that a mesh axis runs over, the one named last changes fastest.
Arguments:
- grads: bfloat16 [8, 1024, 28672], P('dp', 'fsdp')
- block_slot: int32 [28], replicated, may hold values from 0 to 63, as said below
- left_stats: float32 [64, 1024, 1024], P('fsdp', 'dp')
- right_stats: float32 [64, 1024, 1024], P('fsdp', 'dp')
- left_root: bfloat16 [64, 1024, 1024], P('fsdp', 'dp')
- right_root: bfloat16 [64, 1024, 1024], P('fsdp', 'dp')
Outputs:
- left_new: float32 [64, 1024, 1024], P('fsdp', 'dp')
- right_new: float32 [64, 1024, 1024], P('fsdp', 'dp')
- update: bfloat16 [1024, 28672], P('fsdp')
Inputs may be any that keep to these rules, and one draw needn't show every extreme that they name: The entries of block_slot are distinct. Block b's statistics and roots sit in slot block_slot[b], which belongs to the fsdp device of index block_slot[b]; slots that no block names are empty and their statistics pass through unchanged.
All inputs are finite; a program needn't handle non-finite values.
Results may differ from a plain program's by a relative error of at most 0.015.
Values may be sent and summed in bfloat16 or wider, within the bound.
No kernel may reach another device: no remote copies, remote signals or barrier semaphores. Data moves between devices by JAX's collectives and lax.ppermute only.
A program may use at most 64 MiB of HBM per device.

v0:
```python
import jax
import jax.numpy as jnp
from jax import lax
from jax.sharding import Mesh
from jax.sharding import PartitionSpec as P

FSDP = ("fsdp_0", "fsdp_1", "fsdp_2")
epsilon = 1e-06


def per_device(grads, block_slot, left_stats, right_stats, left_root, right_root):
    rows = grads[0]
    row_dev, col_count = rows.shape
    block_size = left_stats.shape[2]
    block_count = col_count // block_size
    shared = left_stats.shape[1]
    replicas = lax.axis_size("dp")
    total_slots = lax.axis_size(FSDP)
    slot_ids = jnp.arange(total_slots, dtype=jnp.int32)
    matches = block_slot[None, :] == slot_ids[:, None]
    filled = jnp.any(matches, axis=1)
    numbers = jnp.arange(block_count, dtype=jnp.int32)
    source = jnp.sum(jnp.where(matches, numbers[None, :], 0), axis=1)
    whole_left = lax.all_gather(left_root[0], "dp", axis=0, tiled=True)
    shares = rows.reshape(row_dev, block_count, replicas, shared).transpose(2, 1, 0, 3)
    shares = shares.reshape(replicas, block_count * row_dev, shared)
    roots = right_root[0].reshape(shared, replicas, shared).transpose(1, 0, 2)
    message = jnp.concatenate([shares, roots], axis=1)
    received = lax.all_to_all(message, "dp", 0, 0, tiled=True)
    summed = jnp.sum(received[:, : block_count * row_dev].astype(jnp.float32), axis=0)
    summed = summed.astype(jnp.bfloat16).reshape(block_count, row_dev, shared)
    right_cols = received[:, block_count * row_dev :]
    outgoing = jnp.where(
        filled[:, None, None], jnp.take(summed, source, axis=0), jnp.zeros((), jnp.bfloat16)
    )
    incoming = lax.all_to_all(outgoing, FSDP, 0, 0, tiled=True)
    mine, whole_left = lax.optimization_barrier((incoming.reshape(block_size, shared), whole_left))
    gradient = lax.all_gather(mine, "dp", axis=1, tiled=True)
    inner = jnp.einsum(
        "rk,kc->rc",
        gradient,
        right_cols.reshape(block_size, shared),
        preferred_element_type=jnp.float32,
    )
    high = lax.reduce_precision(inner, 8, 7)
    low = (inner - high).astype(jnp.bfloat16)
    high = high.astype(jnp.bfloat16)
    both = jnp.einsum(
        "kr,rc->kc", whole_left, high, preferred_element_type=jnp.float32
    ) + jnp.einsum("kr,rc->kc", whole_left, low, preferred_element_type=jnp.float32)
    both = both.astype(jnp.bfloat16).reshape(total_slots, row_dev, shared)
    back = lax.all_to_all(both, FSDP, 0, 0, tiled=True)
    row_start = lax.axis_index("dp") * shared
    own_rows = lax.dynamic_slice_in_dim(gradient, row_start, shared, 0)
    left_new = left_stats + jnp.einsum(
        "rc,kc->rk", own_rows, gradient, preferred_element_type=jnp.float32
    )
    right_new = right_stats + jnp.einsum(
        "rc,rk->ck", mine, gradient, preferred_element_type=jnp.float32
    )
    wide = back.astype(jnp.float32)
    squares = lax.psum(jnp.sum(wide * wide, axis=(1, 2)), FSDP + ("dp",))
    picked = jnp.take(back, block_slot, axis=0)
    full = lax.all_gather(picked, "dp", axis=0, tiled=False)
    factor = lax.rsqrt(jnp.take(squares, block_slot) / (block_size * block_size) + epsilon)
    update = (full.astype(jnp.float32) * factor[None, :, None, None]).astype(jnp.bfloat16)
    update = update.transpose(2, 1, 0, 3).reshape(row_dev, col_count)
    return (left_new, right_new, update)


def solution(mesh):
    split = Mesh(
        mesh.devices.reshape(4, 8, 2, mesh.shape["dp"]), ("fsdp_0", "fsdp_1", "fsdp_2", "dp")
    )
    placed = (
        P("dp", FSDP, None),
        P(),
        P(FSDP, "dp", None),
        P(FSDP, "dp", None),
        P(FSDP, "dp", None),
        P(FSDP, "dp", None),
    )
    return jax.shard_map(
        per_device,
        mesh=split,
        in_specs=placed,
        out_specs=(P(FSDP, "dp", None), P(FSDP, "dp", None), P(FSDP, None)),
        check_vma=False,
    )
```

profile of v0, /device:TPU:2, one launch (start us, length us, event | category | flops | bytes accessed | tf_op | source)
XLA Modules:
  0.0 291.5 jit_solution(8681560645915231170)
XLA Ops:
  7.2 0.0 all-gather.6.cloned.1.call-start
  7.2 0.7 all-gather.6.cloned.1.call-update
  7.9 1.1 copy.24
  9.0 0.2 copy.25
  9.2 1.3 copy.27
  10.5 0.4 copy.23
  10.9 0.0 copy-start.6
  10.9 1.1 pad_maximum_fusion
  12.0 10.3 %all-to-all-start = ((bf16[8,576,128]{2,1,0:T(8,128)(2,1)}), bf16[8,576,128]{2,1,0:T(8,128)(2,1)S(1)}, u32[]{:S(2)}, u32[]{:S(2)}) async-start(bf16[8,576,128]{2,1,0:T(8,128)(2,1)} %pad_maximum_fusion), calls=%async_computation | async-start | bytes 2359296 | tf_op jit(solution)/shard_map/all_to_all | solution.py:29
  22.3 0.0 all-gather.4.cloned.1.call-start
  22.4 0.0 copy-done.6
  22.4 0.1 select_reduce_fusion
  22.5 0.1 fusion.8
  22.6 41.9 %all-to-all-done = bf16[8,576,128]{2,1,0:T(8,128)(2,1)S(1)} async-done(((bf16[8,576,128]{2,1,0:T(8,128)(2,1)}), bf16[8,576,128]{2,1,0:T(8,128)(2,1)S(1)}, u32[]{:S(2)}, u32[]{:S(2)}) %all-to-all-start) | async-done | bytes 1179680 | tf_op jit(solution)/shard_map/all_to_all | solution.py:29
  64.5 0.1 slice_reduce_fusion
  64.6 0.6 gather_fusion
  65.3 0.2 select_select_fusion
  65.5 22.4 %all_to_all.15 = bf16[64,16,128]{2,1,0:T(8,128)(2,1)} all-to-all(bf16[64,16,128]{2,1,0:T(8,128)(2,1)S(1)} %select_select_fusion), channel_id=1, replica_groups=mesh['fsdp_0'=4,'fsdp_1'=8,'fsdp_2'=2,'dp'=8] {'fsdp_0','fsdp_1','fsdp_2'}, dimensions={0} | all-to-all | bytes 524288 | tf_op jit(solution)/shard_map/all_to_all | solution.py:36
  87.9 0.0 all-gather.6.cloned.1.call-done
  87.9 0.0 copy-start.1
  87.9 0.0 all-gather.4.cloned.1.call-update
  88.0 42.8 %all-gather.4.cloned.1.call-done = bf16[1024,1024]{1,0:T(8,128)(2,1)} async-done(((bf16[1024,128]{1,0:T(8,128)(2,1)}), bf16[1024,1024]{1,0:T(8,128)(2,1)}) %all-gather.4.cloned.1.call-update) | async-done | bytes 2097168 | tf_op jit(solution)/shard_map/all_gather | solution.py:38
  130.7 2.3 fusion.11
  133.0 0.0 copy-done.1
  133.0 0.0 copy-start.2
  133.0 0.7 fusion.6
  133.8 0.9 copy-done.2
  134.6 0.0 copy-start
  134.6 0.0 copy-start.4
  134.6 1.4 fusion.2
  136.1 10.4 %all-to-all-start.2 = ((bf16[64,16,128]{2,1,0:T(8,128)(2,1)}), bf16[64,16,128]{2,1,0:T(8,128)(2,1)S(1)}, u32[]{:S(2)}, u32[]{:S(2)}) async-start(bf16[64,16,128]{2,1,0:T(8,128)(2,1)} %bitcast.12), calls=%async_computation.2 | async-start | bytes 524288 | tf_op jit(solution)/shard_map/all_to_all | solution.py:52
  146.5 0.0 copy-done
  146.5 0.0 copy-done.4
  146.5 0.0 copy-start.5
  146.5 1.6 fusion
  148.1 0.0 copy-done.3
  148.1 0.0 copy-done.5
  148.1 1.3 fusion.1
  149.4 8.6 %all-to-all-done.2 = bf16[64,16,128]{2,1,0:T(8,128)(2,1)S(1)} async-done(((bf16[64,16,128]{2,1,0:T(8,128)(2,1)}), bf16[64,16,128]{2,1,0:T(8,128)(2,1)S(1)}, u32[]{:S(2)}, u32[]{:S(2)}) %all-to-all-start.2) | async-done | bytes 262176 | tf_op jit(solution)/shard_map/all_to_all | solution.py:52
  158.0 0.6 multiply_reduce_fusion
  158.6 96.1 %psum.7 = f32[64]{0:T(128)S(1)} all-reduce(f32[64]{0:T(128)S(1)} %multiply_reduce_fusion), channel_id=1, replica_groups=mesh['fsdp_0'=4,'fsdp_1'=8,'fsdp_2'=2,'dp'=8] {'fsdp_0','fsdp_1','fsdp_2..., use_global_device_ids=true, to_apply=%region_4.5 | all-reduce | flops 64 | bytes 512 | tf_op jit(solution)/shard_map/psum | solution.py:62
  254.6 0.7 gather_fusion.2
  255.3 0.6 gather_fusion.1
  255.9 0.1 bitcast_select_fusion
  256.0 26.4 %all_gather.12 = bf16[8,28,16,128]{3,2,1,0:T(8,128)(2,1)S(1)} all-gather(bf16[1,28,16,128]{3,2,1,0:T(8,128)(2,1)S(1)} %bitcast_select_fusion), channel_id=1, replica_groups=mesh['fsdp_0'=4,'fsdp_1'=8,'fsdp_2'=2,'dp'=8] {'dp'}, dimensions={0}, use_global_device_ids=true | all-gather | bytes 1032192 | tf_op jit(solution)/shard_map/all_gather | solution.py:64
  282.5 0.3 fusion.3
  282.8 0.6 copy.26
  283.4 1.3 copy.30
  (8 shorter events, 0.1 us)
Async XLA Ops:
  7.2 80.7 %all-gather.6.cloned.1.call-start = ((), (), s32[]{:S(2)}) async-start(), calls=%async_computation.4 | async-start | bytes 2359296 | tf_op jit(solution)/shard_map/all_gather | solution.py:24
  10.9 11.5 %copy-start.6 = (s32[28]{0:T(128)S(1)}, s32[28]{0:T(128)}, u32[]{:S(2)}) copy-start(s32[28]{0:T(128)} %param.7) | copy-start | bytes 340
  12.0 52.5 %all-to-all-start = ((bf16[8,576,128]{2,1,0:T(8,128)(2,1)}), bf16[8,576,128]{2,1,0:T(8,128)(2,1)S(1)}, u32[]{:S(2)}, u32[]{:S(2)}) async-start(bf16[8,576,128]{2,1,0:T(8,128)(2,1)} %pad_maximum_fusion), calls=%async_computation | async-start | bytes 2359296 | tf_op jit(solution)/shard_map/all_to_all | solution.py:29
  22.3 108.4 %all-gather.4.cloned.1.call-start = ((), (), s32[]{:S(2)}) async-start(), calls=%async_computation.3 | async-start | bytes 2359296 | tf_op jit(solution)/shard_map/all_gather | solution.py:38
  87.9 45.1 %copy-start.1 = (bf16[1,1024,1024]{2,1,0:T(8,128)(2,1)S(1)}, bf16[1,1024,1024]{2,1,0:T(8,128)(2,1)}, u32[]{:S(2)}) copy-start(bf16[1,1024,1024]{2,1,0:T(8,128)(2,1)} %all-gather.6.cloned.1.call-done) | copy-start | bytes 6291460
  133.0 1.6 copy-start.2
  134.6 11.8 %copy-start = (bf16[1024,1024]{1,0:T(8,128)(2,1)S(1)}, bf16[1024,1024]{1,0:T(8,128)(2,1)}, u32[]{:S(2)}) copy-start(bf16[1024,1024]{1,0:T(8,128)(2,1)} %all-gather.4.cloned.1.call-done) | copy-start | bytes 6291460
  134.6 11.9 %copy-start.4 = (f32[1,128,1024]{2,1,0:T(8,128)S(1)}, f32[1,128,1024]{2,1,0:T(8,128)}, u32[]{:S(2)}) copy-start(f32[1,128,1024]{2,1,0:T(8,128)} %param.8) | copy-start | bytes 1572868
  136.1 12.1 %copy-start.3 = (bf16[64,16,128]{2,1,0:T(8,128)(2,1)S(1)}, bf16[64,16,128]{2,1,0:T(8,128)(2,1)}, u32[]{:S(2)}) copy-start(bf16[64,16,128]{2,1,0:T(8,128)(2,1)} %all_to_all.15) | copy-start | bytes 786436
  136.1 21.9 %all-to-all-start.2 = ((bf16[64,16,128]{2,1,0:T(8,128)(2,1)}), bf16[64,16,128]{2,1,0:T(8,128)(2,1)S(1)}, u32[]{:S(2)}, u32[]{:S(2)}) async-start(bf16[64,16,128]{2,1,0:T(8,128)(2,1)} %bitcast.12), calls=%async_computation.2 | async-start | bytes 524288 | tf_op jit(solution)/shard_map/all_to_all | solution.py:52
  146.5 1.7 copy-start.5
Sparse Core Ops, SparseCore 0:
  10.1 64.5 all-gather.5
  88.0 42.6 all-gather.3
where the time goes:
time: 292 us; the launch traced here: 291 us
  blocking collectives  145 us (50%)
  waiting for transfers between devices  94 us (32%)
  starting transfers between devices  20.8 us (7%)
  between operations  14.2 us (5%)
  local copies, waits for them, and re-layouts  7.68 us (3%)
  matrix products  7.32 us (3%)
    psum x1, blocking collectives, per_device(): squares = lax.psum(jnp.sum(wide * wide, axis=(1, 2)), FSDP + ('dp',))  96.1 us
    all_gather x1, waiting for transfers between devices, per_device(): gradient = lax.all_gather(mine, 'dp', axis=1, tiled=True)  42.8 us
    all_to_all x1, waiting for transfers between devices, per_device(): received = lax.all_to_all(message, 'dp', 0, 0, tiled=True)  41.9 us
    all_gather x1, blocking collectives, per_device(): full = lax.all_gather(picked, 'dp', axis=0, tiled=False)  26.4 us
    all_to_all x1, blocking collectives, per_device(): incoming = lax.all_to_all(outgoing, FSDP, 0, 0, tiled=True)  22.4 us
    all_to_all x1, starting transfers between devices, per_device(): back = lax.all_to_all(both, FSDP, 0, 0, tiled=True)  10.4 us
    all_to_all x1, starting transfers between devices, per_device(): received = lax.all_to_all(message, 'dp', 0, 0, tiled=True)  10.3 us
    all_to_all x1, waiting for transfers between devices, per_device(): back = lax.all_to_all(both, FSDP, 0, 0, tiled=True)  8.59 us
  transfers between devices with their start and end apart: 4, of which 3 were waited for; matrix products, arithmetic and copies ran while one was open for 3% of the time, Pallas kernels for 0%

commit v1 on v0

--- a/solution.py
+++ b/solution.py
@@ -35,7 +35,9 @@
     )
     incoming = lax.all_to_all(outgoing, FSDP, 0, 0, tiled=True)
     mine, whole_left = lax.optimization_barrier((incoming.reshape(block_size, shared), whole_left))
-    gradient = lax.all_gather(mine, "dp", axis=1, tiled=True)
+    gradient = jnp.concatenate(
+        lax.all_to_all(jnp.stack([mine] * lax.axis_size("dp")), "dp", 0, 0), axis=1
+    )
     inner = jnp.einsum(
         "rk,kc->rc",
         gradient,

time: 292 us -> 298 us (1.021)
  waiting for transfers between devices: 94 us -> 97.5 us
  local copies, waits for them, and re-layouts: 7.68 us -> 10.9 us
    all_to_all x0 -> x1, waiting for transfers between devices: none -> 51.7 us  [per_device(): lax.all_to_all(jnp.stack([mine] * lax.axis_size('dp')), 'dp', 0, 0)]
    all_gather x1 -> x0, waiting for transfers between devices: 42.8 us -> none  [per_device(): gradient = lax.all_gather(mine, 'dp', axis=1, tiled=True)]
    all_to_all x1, waiting for transfers between devices: 8.59 us -> 4.15 us  [per_device(): back = lax.all_to_all(both, FSDP, 0, 0, tiled=True)]
    all_to_all x1, starting transfers between devices: 10.4 us -> 6.3 us  [per_device(): back = lax.all_to_all(both, FSDP, 0, 0, tiled=True)]
    all_to_all x0 -> x1, starting transfers between devices: none -> 3.6 us  [per_device(): lax.all_to_all(jnp.stack([mine] * lax.axis_size('dp')), 'dp', 0, 0)]
  transfers between devices with their start and end apart: 4 -> 4, of which waited for: 3 -> 3; matrix products, arithmetic and copies ran while one was open for 3% -> 4% of each run, Pallas kernels for 0% -> 0%
where the time goes in v1:
time: 298 us; the launch traced here: 297 us
  blocking collectives  144 us (48%)
  waiting for transfers between devices  97.5 us (33%)
  starting transfers between devices  20.3 us (7%)
  between operations  14.2 us (5%)
  local copies, waits for them, and re-layouts  10.9 us (4%)
  matrix products  7.57 us (3%)
    psum x1, blocking collectives, per_device(): squares = lax.psum(jnp.sum(wide * wide, axis=(1, 2)), FSDP + ('dp',))  95.3 us
    all_to_all x1, waiting for transfers between devices, per_device(): lax.all_to_all(jnp.stack([mine] * lax.axis_size('dp')), 'dp', 0, 0)  51.7 us
    all_to_all x1, waiting for transfers between devices, per_device(): received = lax.all_to_all(message, 'dp', 0, 0, tiled=True)  41 us
    all_gather x1, blocking collectives, per_device(): full = lax.all_gather(picked, 'dp', axis=0, tiled=False)  26.6 us
    all_to_all x1, blocking collectives, per_device(): incoming = lax.all_to_all(outgoing, FSDP, 0, 0, tiled=True)  22.2 us
    all_to_all x1, starting transfers between devices, per_device(): received = lax.all_to_all(message, 'dp', 0, 0, tiled=True)  10.3 us
    all_to_all x1, starting transfers between devices, per_device(): back = lax.all_to_all(both, FSDP, 0, 0, tiled=True)  6.3 us
  transfers between devices with their start and end apart: 4, of which 3 were waited for; matrix products, arithmetic and copies ran while one was open for 4% of the time, Pallas kernels for 0%

profile of v1, /device:TPU:2, one launch (start us, length us, event | category | flops | bytes accessed | tf_op | source)
XLA Modules:
  0.0 297.1 jit_solution(17274016032011043018)
XLA Ops:
  7.2 0.0 copy-start.4
  7.2 0.0 all-gather.3.cloned.1.call-start
  7.2 0.7 all-gather.3.cloned.1.call-update
  7.9 1.3 copy.30
  9.2 0.4 copy.25
  9.6 0.0 copy-done.4
  9.6 0.2 copy.26
  9.8 0.2 copy.27
  9.9 0.0 copy-start.5
  10.0 1.1 pad_maximum_fusion
  11.1 10.3 %all-to-all-start = ((bf16[8,576,128]{2,1,0:T(8,128)(2,1)}), bf16[8,576,128]{2,1,0:T(8,128)(2,1)S(1)}, u32[]{:S(2)}, u32[]{:S(2)}) async-start(bf16[8,576,128]{2,1,0:T(8,128)(2,1)} %pad_maximum_fusion), calls=%async_computation | async-start | bytes 2359296 | tf_op jit(solution)/shard_map/all_to_all | solution.py:29
  21.4 0.0 copy-done.5
  21.4 0.1 select_reduce_fusion
  21.5 0.1 fusion.9
  21.6 41.0 %all-to-all-done = bf16[8,576,128]{2,1,0:T(8,128)(2,1)S(1)} async-done(((bf16[8,576,128]{2,1,0:T(8,128)(2,1)}), bf16[8,576,128]{2,1,0:T(8,128)(2,1)S(1)}, u32[]{:S(2)}, u32[]{:S(2)}) %all-to-all-start) | async-done | bytes 1179680 | tf_op jit(solution)/shard_map/all_to_all | solution.py:29
  62.6 0.1 slice_reduce_fusion
  62.7 0.6 gather_fusion
  63.4 0.2 select_select_fusion
  63.6 22.2 %all_to_all.20 = bf16[64,16,128]{2,1,0:T(8,128)(2,1)S(1)} all-to-all(bf16[64,16,128]{2,1,0:T(8,128)(2,1)S(1)} %select_select_fusion), channel_id=1, replica_groups=mesh['fsdp_0'=4,'fsdp_1'=8,'fsdp_2'=2,'dp'=8] {'fsdp_0','fsdp_1','fsdp_2'}, dimensions={0} | all-to-all | bytes 524288 | tf_op jit(solution)/shard_map/all_to_all | solution.py:36
  85.8 0.0 all-gather.3.cloned.1.call-done
  85.8 1.6 stack.2
  87.4 3.6 %all-to-all-start.2 = ((bf16[8,1024,128]{2,1,0:T(8,128)(2,1)}), bf16[8,1024,128]{2,1,0:T(8,128)(2,1)S(1)}, u32[]{:S(2)}, u32[]{:S(2)}) async-start(bf16[8,1024,128]{2,1,0:T(8,128)(2,1)} %stack.2), calls=%async_computation.2 | async-start | bytes 4194304 | tf_op jit(solution)/shard_map/all_to_all | solution.py:39
  91.0 51.7 %all-to-all-done.2 = bf16[8,1024,128]{2,1,0:T(8,128)(2,1)S(1)} async-done(((bf16[8,1024,128]{2,1,0:T(8,128)(2,1)}), bf16[8,1024,128]{2,1,0:T(8,128)(2,1)S(1)}, u32[]{:S(2)}, u32[]{:S(2)}) %all-to-all-start.2) | async-done | bytes 2097184 | tf_op jit(solution)/shard_map/all_to_all | solution.py:39
  142.7 0.0 copy-start.1
  142.7 0.7 convolution_bitcast_fusion
  143.4 0.9 copy-done.1
  144.3 0.7 fusion.6
  145.0 1.4 fusion.2
  146.4 6.3 %all-to-all-start.3 = ((bf16[64,16,128]{2,1,0:T(8,128)(2,1)}), bf16[64,16,128]{2,1,0:T(8,128)(2,1)S(1)}, u32[]{:S(2)}, u32[]{:S(2)}) async-start(bf16[64,16,128]{2,1,0:T(8,128)(2,1)} %bitcast.14), calls=%async_computation.3 | async-start | bytes 524288 | tf_op jit(solution)/shard_map/all_to_all | solution.py:54
  152.7 0.0 copy-start.2
  152.7 2.6 copy.28
  155.3 0.0 copy-start
  155.3 0.0 copy-start.3
  155.3 0.0 copy-done.2
  155.3 3.1 %fusion = f32[1,128,1024]{2,1,0:T(8,128)} fusion(f32[1,128,1024]{2,1,0:T(8,128)S(1)} %copy-done.2, bf16[1024,1024]{0,1:T(8,128)(2,1)} %bitcast.46, s32[]{:T(128)S(6)} %select_n.60), kind=kOutput, calls=%fused_computation.8 | convolution fusion | flops 268566528 | bytes 3407876 | tf_op jit(solution)/shard_map/rc,kc->rk/dot_general | solution.py:57
  158.4 0.0 copy-done
  158.4 0.0 copy-done.3
  158.4 1.6 fusion.1
  160.1 4.2 %all-to-all-done.3 = bf16[64,16,128]{2,1,0:T(8,128)(2,1)S(1)} async-done(((bf16[64,16,128]{2,1,0:T(8,128)(2,1)}), bf16[64,16,128]{2,1,0:T(8,128)(2,1)S(1)}, u32[]{:S(2)}, u32[]{:S(2)}) %all-to-all-start.3) | async-done | bytes 262176 | tf_op jit(solution)/shard_map/all_to_all | solution.py:54
  164.2 0.6 multiply_reduce_fusion
  164.8 95.3 %psum.7 = f32[64]{0:T(128)S(1)} all-reduce(f32[64]{0:T(128)S(1)} %multiply_reduce_fusion), channel_id=1, replica_groups=mesh['fsdp_0'=4,'fsdp_1'=8,'fsdp_2'=2,'dp'=8] {'fsdp_0','fsdp_1','fsdp_2..., use_global_device_ids=true, to_apply=%region_4.5 | all-reduce | flops 64 | bytes 512 | tf_op jit(solution)/shard_map/psum | solution.py:64
  260.1 0.7 gather_fusion.2
  260.8 0.6 gather_fusion.1
  261.4 0.1 bitcast_select_fusion
  261.5 26.6 %all_gather.8 = bf16[8,28,16,128]{3,2,1,0:T(8,128)(2,1)S(1)} all-gather(bf16[1,28,16,128]{3,2,1,0:T(8,128)(2,1)S(1)} %bitcast_select_fusion), channel_id=1, replica_groups=mesh['fsdp_0'=4,'fsdp_1'=8,'fsdp_2'=2,'dp'=8] {'dp'}, dimensions={0}, use_global_device_ids=true | all-gather | bytes 1032192 | tf_op jit(solution)/shard_map/all_gather | solution.py:66
  288.1 0.3 fusion.3
  288.4 0.6 copy.29
  289.0 1.3 copy.33
  (6 shorter events, 0.0 us)
Async XLA Ops:
  7.2 2.4 copy-start.4
  7.2 78.6 %all-gather.3.cloned.1.call-start = ((), (), s32[]{:S(2)}) async-start(), calls=%async_computation.4 | async-start | bytes 2359296 | tf_op jit(solution)/shard_map/all_gather | solution.py:24
  9.9 11.4 %copy-start.5 = (s32[28]{0:T(128)S(1)}, s32[28]{0:T(128)}, u32[]{:S(2)}) copy-start(s32[28]{0:T(128)} %param.7) | copy-start | bytes 340
  11.1 51.5 %all-to-all-start = ((bf16[8,576,128]{2,1,0:T(8,128)(2,1)}), bf16[8,576,128]{2,1,0:T(8,128)(2,1)S(1)}, u32[]{:S(2)}, u32[]{:S(2)}) async-start(bf16[8,576,128]{2,1,0:T(8,128)(2,1)} %pad_maximum_fusion), calls=%async_computation | async-start | bytes 2359296 | tf_op jit(solution)/shard_map/all_to_all | solution.py:29
  87.4 55.3 %all-to-all-start.2 = ((bf16[8,1024,128]{2,1,0:T(8,128)(2,1)}), bf16[8,1024,128]{2,1,0:T(8,128)(2,1)S(1)}, u32[]{:S(2)}, u32[]{:S(2)}) async-start(bf16[8,1024,128]{2,1,0:T(8,128)(2,1)} %stack.2), calls=%async_computation.2 | async-start | bytes 4194304 | tf_op jit(solution)/shard_map/all_to_all | solution.py:39
  142.7 1.6 copy-start.1
  146.4 17.8 %all-to-all-start.3 = ((bf16[64,16,128]{2,1,0:T(8,128)(2,1)}), bf16[64,16,128]{2,1,0:T(8,128)(2,1)S(1)}, u32[]{:S(2)}, u32[]{:S(2)}) async-start(bf16[64,16,128]{2,1,0:T(8,128)(2,1)} %bitcast.14), calls=%async_computation.3 | async-start | bytes 524288 | tf_op jit(solution)/shard_map/all_to_all | solution.py:54
  152.7 2.6 copy-start.2
  155.3 3.1 %copy-start = (bf16[1024,8,128]{0,2,1:T(8,128)(2,1)S(1)}, bf16[1024,8,128]{0,2,1:T(8,128)(2,1)}, u32[]{:S(2)}) copy-start(bf16[1024,8,128]{0,2,1:T(8,128)(2,1)} %copy.28) | copy-start | bytes 6291460
  155.3 3.1 %copy-start.3 = (f32[1,128,1024]{2,1,0:T(8,128)S(1)}, f32[1,128,1024]{2,1,0:T(8,128)}, u32[]{:S(2)}) copy-start(f32[1,128,1024]{2,1,0:T(8,128)} %param.9) | copy-start | bytes 1572868
Sparse Core Ops, SparseCore 0:
  10.1 63.5 all-gather.2
